TPU v7x, 32 devices: a whole 2x2x4 slice. The times are simulated.
32 devices in a mesh: xfer: 8 (over y, x, core), head: 4 (over z).
Axes of the slice: x: 2, y: 2, z: 4, core: 2. Of those that a mesh axis runs over, the one named last changes fastest.
Arguments:
- kv_pool: bfloat16 [256, 64, 576], P(('xfer', 'head')), may hold values from -8 to 8
- lengths: int32 [64], replicated, may hold values from 2 to 1600, as said below
- start_device: int32 [64], replicated, may hold values from 0 to 31, as said below
- page_table: int32 [64, 32], replicated, may hold values from 0 to 7, as said below
- queries: bfloat16 [128, 128, 192], P('xfer', 'head'), may hold values from -100 to 100
- new_latent: bfloat16 [128, 576], P('xfer'), may hold values from -100 to 100
- key_up: bfloat16 [128, 128, 512], P('head'), may hold values from -0.25 to 0.25
- value_up: bfloat16 [128, 512, 128], P('head'), may hold values from -0.25 to 0.25
- out_proj: bfloat16 [16384, 7168], P('head', 'xfer'), may hold values from -0.046875 to 0.046875
Outputs:
- attn_out: bfloat16 [128, 7168], P('head', 'xfer')
Inputs may be any that keep to these rules, and one draw needn't show every extreme that they name: `lengths`: request r belongs to decode owner xfer index r // 8. The pages of one owner's requests number 32 // 2 to 32, exactly 32 for some owner, so one owner has at most one page on any device. Page j of request r lies on device (start_device[r] + j) mod 32. `page_table`: entries past a request's pages are 0; two pages on one device never share a slot.
All inputs are finite; a program needn't handle non-finite values.
Results may differ from a plain program's by a relative error of at most 0.0058.
Values may be sent and summed in bfloat16 or wider, within the bound.
No kernel may reach another device: no remote copies, remote signals or barrier semaphores. Data moves between devices by JAX's collectives and lax.ppermute only.
A program may use at most 128 MiB of HBM per device.

v0:
```python
import functools

import jax
import jax.numpy as jnp
from jax import lax
from jax.experimental import pallas as pl
from jax.experimental.pallas import tpu as pltpu
from jax.sharding import PartitionSpec as P


STEPS = 2
HIDDEN = -1e30
F32 = jnp.float32
BF16 = jnp.bfloat16
ANY = pl.BlockSpec(memory_space=pl.ANY)
HBM = pl.BlockSpec(memory_space=pltpu.HBM)
VMEM = pl.BlockSpec(memory_space=pltpu.VMEM)
SMEM = pl.BlockSpec(memory_space=pltpu.SMEM)


def gather_kernel(cfg, idx, lengths_hbm, starts_hbm, table_hbm, pool_hbm, other, same, *scratch):
    devices, groups, per_owner = cfg
    lengths, starts, table, pool, sem = scratch
    copies = [
        pltpu.make_async_copy(src, dst, sem.at[i])
        for i, (src, dst) in enumerate(
            ((lengths_hbm, lengths), (starts_hbm, starts), (table_hbm, table), (pool_hbm, pool))
        )
    ]
    for c in copies:
        c.start()
    page_len = pool.shape[1]
    half = other.shape[0]
    me, z = idx[0], idx[1]
    column = lax.broadcasted_iota(jnp.int32, table.shape, 0)
    request = lax.broadcasted_iota(jnp.int32, table.shape, 1)
    for c in copies[:3]:
        c.wait()
    at = starts[...] + column
    here = jnp.where(at >= devices, at - devices, at) == me * groups + z
    here = here & (column * page_len < lengths[...])
    slots = jnp.where(here, table[...], 0)
    owner = request // per_owner
    chosen = []
    for flip in (1, 0):
        for m in range(half):
            chosen.append(jnp.sum(jnp.where(owner == me ^ (2 * m) ^ flip, slots, 0)))
    copies[3].wait()
    for m in range(half):
        other[m] = pool[chosen[m]]
        same[m] = pool[chosen[half + m]]


def gather_pages(idx, pool, lengths, starts, table, groups):
    requests, _ = table.shape
    owners = pool.shape[0]
    half = jax.ShapeDtypeStruct((owners // 2,) + pool.shape[1:], pool.dtype)
    cfg = (owners * groups, groups, requests // owners)
    args = (lengths.reshape(1, -1), starts.reshape(1, -1), table.T, pool)
    args = tuple(pltpu.with_memory_space_constraint(x, pltpu.HBM) for x in args)
    return pl.pallas_call(
        functools.partial(gather_kernel, cfg),
        out_shape=[half] * 2,
        in_specs=[SMEM] + [HBM] * 4,
        out_specs=[VMEM] * 2,
        scratch_shapes=[pltpu.VMEM(x.shape, x.dtype) for x in args]
        + [pltpu.SemaphoreType.DMA((4,))],
        compiler_params=pltpu.CompilerParams(vmem_limit_bytes=16 << 20),
    )(idx, *args)


def pack_kernel(same, part, ring, *outs):
    last = len(outs)
    for i, source in enumerate((same, part)):
        ring[i] = source[0]
        ring[2 + i] = source[last]
        for m, out in enumerate(outs, 1):
            out[i] = source[m]


def pack_pages(same, part):
    pair = jax.ShapeDtypeStruct((2,) + same.shape[1:], same.dtype)
    ring = jax.ShapeDtypeStruct((4,) + same.shape[1:], same.dtype)
    count = same.shape[0] - 1
    return pl.pallas_call(
        pack_kernel,
        out_shape=[ring] + [pair] * count,
        in_specs=[VMEM] * 2,
        out_specs=[VMEM] * (count + 1),
        compiler_params=pltpu.CompilerParams(vmem_limit_bytes=16 << 20),
    )(same, part)


def absorb_kernel(queries_hbm, key_up_hbm, out, queries, key_up, flat, rope, sem):
    rows, heads, dim = queries.shape
    nope, rank = key_up.shape[1:]
    pieces = sem.shape[0] - 1
    n = heads // pieces
    copies = [pltpu.make_async_copy(queries_hbm, queries, sem.at[pieces])]
    for i in range(pieces):
        at = pl.ds(i * n, n)
        copies.append(pltpu.make_async_copy(key_up_hbm.at[at], key_up.at[at], sem.at[i]))
    for c in copies:
        c.start()
    copies[0].wait()
    q = queries[...].reshape(rows * heads, dim).astype(F32)
    flat[...] = q[:, :nope]
    rope[:, : dim - nope] = q[:, nope:]
    for h in range(heads):
        if h % n == 0:
            copies[1 + h // n].wait()
        pick = pl.ds(h, rows, stride=heads)
        at = pl.ds(h * rows, rows)
        out[at, :rank] = jnp.dot(
            flat[pick, :].astype(BF16), key_up[h], preferred_element_type=F32
        ).astype(BF16)
        out[at, rank:] = rope[pick, :][:, : dim - nope].astype(BF16)


def absorb(queries, key_up):
    rows, heads, dim = queries.shape
    width = key_up.shape[2] + dim - key_up.shape[1]
    args = tuple(pltpu.with_memory_space_constraint(x, pltpu.HBM) for x in (queries, key_up))
    return pl.pallas_call(
        absorb_kernel,
        out_shape=jax.ShapeDtypeStruct((heads * rows, width), BF16),
        in_specs=[HBM] * 2,
        out_specs=VMEM,
        scratch_shapes=[
            pltpu.VMEM(queries.shape, queries.dtype),
            pltpu.VMEM(key_up.shape, key_up.dtype),
            pltpu.VMEM((rows * heads, key_up.shape[1]), F32),
            pltpu.VMEM((rows * heads, pl.cdiv(dim - key_up.shape[1], 128) * 128), F32),
            pltpu.SemaphoreType.DMA((5,)),
        ],
        compiler_params=pltpu.CompilerParams(vmem_limit_bytes=16 << 20),
        cost_estimate=pl.CostEstimate(
            flops=2 * rows * key_up.size, transcendentals=0, bytes_accessed=2 * key_up.size
        ),
    )(*args)


def row_chunks(heads, rows):
    size = max(1, 512 // rows)
    return [(h, min(size, heads - h)) for h in range(0, heads, size)]


def attend(q, parts, scale, lat_rank, old):
    n = q.shape[0]
    scores = []
    for keys, bias in parts:
        rows = bias.shape[0]
        s = lax.dot_general(q, keys, (((1,), (1,)), ((), ())), preferred_element_type=F32)
        scores.append((s.reshape(n // rows, rows, -1) * scale + bias[None]).reshape(n, -1))
    m = functools.reduce(jnp.maximum, [jnp.max(s, axis=-1, keepdims=True) for s in scores])
    if old is not None:
        m = jnp.maximum(old[0], m)
    l, acc = 0.0, 0.0
    for s, (keys, _) in zip(scores, parts):
        w = jnp.exp(s - m)
        l = l + jnp.sum(w, axis=-1, keepdims=True)
        acc = acc + jnp.dot(w.astype(BF16), keys[:, :lat_rank], preferred_element_type=F32)
    if old is not None:
        keep = jnp.exp(old[0] - m)
        l = l + old[1] * keep
        acc = acc + old[2] * keep
    return m, l, acc


def fill_bias(cfg, idx, lengths, starts, bias):
    devices, groups, per_owner, page_len = cfg
    rows, width = bias.shape[1:]
    tile = max(128, page_len)
    lane = lax.broadcasted_iota(jnp.int32, (rows, tile), 1)
    request = lax.broadcasted_iota(jnp.int32, (rows, tile), 0) // STEPS
    me = idx[0]

    def one(i, _):
        plane, t = i // (width // tile), lax.rem(i, width // tile)
        limit = jnp.zeros((rows, tile), jnp.int32)
        for p in range(tile // page_len):
            home = (me ^ (t * (tile // page_len) + p)) * groups + plane
            for r in range(per_owner):
                at = home - starts[me * per_owner + r]
                at = jnp.where(at < 0, at + devices, at)
                seen = lengths[me * per_owner + r] - (at - p) * page_len
                limit = jnp.where((request == r) & (lane // page_len == p), seen, limit)
        bias[plane, :, pl.ds(pl.multiple_of(t * tile, tile), tile)] = jnp.where(
            lane < limit, 0.0, HIDDEN
        ).astype(F32)
        return 0

    lax.fori_loop(0, groups * (width // tile), one, 0)


def stage_kernel(cfg, *rest):
    heads, rows, lat_rank, scale, counts, first, last, hops, geometry, skips = cfg
    rest = list(rest)

    def take(n):
        out = rest[:n]
        del rest[:n]
        return out

    idx, q = take(2)
    if first:
        lengths, starts, fresh = take(3)
    else:
        bias, m_in, l_in, acc_in = take(4)
    if last:
        (value_up,) = take(1)
    blocks = [list(zip(take(len(c)), c)) for c in counts]
    if last:
        (out,) = take(1)
    else:
        m_s, l_s, acc_s = take(3)
    if first:
        (bias,) = take(1)
        fill_bias(geometry, idx, lengths, starts, bias)
    groups = geometry[1]
    z = idx[1]
    parts = []
    if first:
        row = lax.broadcasted_iota(jnp.int32, (rows, rows), 0)
        col = lax.broadcasted_iota(jnp.int32, (rows, rows), 1)
        ok = (row // STEPS == col // STEPS) & (col <= row)
        parts.append((fresh[...], jnp.where(ok, 0.0, HIDDEN).astype(F32)))
    for hop, skip, block in zip(hops, skips, blocks):
        plane = lax.rem(z + groups - hop, groups)
        at = skip
        for ref, pages in block:
            n = pages * ref.shape[1]
            parts.append((ref[:pages].reshape(n, -1), bias[plane, :, at : at + n]))
            at += n
    for h, n in row_chunks(heads, rows):
        at = pl.ds(h * rows, n * rows)
        old = None if first else (m_in[at], l_in[at], acc_in[at])
        m, l, acc = attend(q[at], parts, scale, lat_rank, old)
        if last:
            latent = (acc * (1.0 / l)).astype(BF16).reshape(n, rows, lat_rank)
            vdim = value_up.shape[-1]
            for i in range(n):
                o = jnp.dot(latent[i], value_up[h + i], preferred_element_type=F32)
                out[:, (h + i) * vdim : (h + i + 1) * vdim] = o.astype(BF16)
        else:
            m_s[at], l_s[at], acc_s[at] = m, l, acc


def stage(
    idx, q, blocks, hops, dims, geometry, fresh=None, state=None, value_up=None, skips=(0, 0)
):
    heads, rows, lat_rank, scale = dims
    first, last = fresh is not None, value_up is not None
    args, specs = [idx, q], [SMEM, VMEM]
    if first:
        args += list(fresh)
        specs += [SMEM, SMEM, VMEM]
    else:
        args += list(state)
        specs += [VMEM] * 4
    if last:
        args.append(value_up)
        specs.append(VMEM)
    for block in blocks:
        args += [x for x, _ in block]
        specs += [VMEM] * len(block)
    tokens = sum(n for _, n in blocks[0]) * geometry[3]
    total = sum(n for b in blocks for _, n in b) * geometry[3]
    if last:
        out_shape = jax.ShapeDtypeStruct((rows, heads * value_up.shape[2]), BF16)
        out_specs = VMEM
    else:
        out_shape = [
            jax.ShapeDtypeStruct((heads * rows, 1), F32),
            jax.ShapeDtypeStruct((heads * rows, 1), F32),
            jax.ShapeDtypeStruct((heads * rows, lat_rank), F32),
        ]
        if first:
            out_shape.append(jax.ShapeDtypeStruct((geometry[1], rows, tokens), F32))
        out_specs = [VMEM] * len(out_shape)
    cfg = (
        heads, rows, lat_rank, scale, tuple(tuple(n for _, n in b) for b in blocks), first, last, tuple(hops),
        geometry, skips,
    )
    work = 2 * heads * rows * total * (q.shape[1] + lat_rank)
    return pl.pallas_call(
        functools.partial(stage_kernel, cfg),
        out_shape=out_shape,
        in_specs=specs,
        out_specs=out_specs,
        compiler_params=pltpu.CompilerParams(vmem_limit_bytes=24 << 20),
        cost_estimate=pl.CostEstimate(flops=work, transcendentals=0, bytes_accessed=4 << 20),
    )(*args)


def project_kernel(masks, groups, idx, *rest):
    blocks = rest[: len(masks)]
    w = rest[len(masks)]
    outs = rest[len(masks) + 1 : len(masks) + 1 + groups]
    lhs, acc = rest[len(masks) + 1 + groups :]
    rows = blocks[0].shape[0]
    cols = w.shape[1]
    me, z = idx[0], idx[1]
    for mask, block in zip(masks, blocks):
        lhs[pl.ds(pl.multiple_of((me ^ mask) * rows, rows), rows)] = block[...]
    for c in range(0, cols, 256):
        n = min(256, cols - c)
        acc[:, c : c + n] = jnp.dot(lhs[...], w[:, c : c + n], preferred_element_type=F32)
        for j, out in enumerate(outs):
            k = out.shape[0]
            at = pl.multiple_of((z ^ j) * k, k)
            out[:, c : c + n] = acc[pl.ds(at, k), c : c + n].astype(out.dtype)


def project(idx, masks, blocks, w, groups):
    rows, depth = blocks[0].shape
    total = rows * len(blocks)
    cols = w.shape[1]
    chunk = total // groups
    outs = [jax.ShapeDtypeStruct((chunk, cols), F32 if j == 0 else BF16) for j in range(groups)]
    return pl.pallas_call(
        functools.partial(project_kernel, tuple(masks), groups),
        out_shape=outs,
        in_specs=[SMEM] + [VMEM] * (len(blocks) + 1),
        out_specs=[VMEM] * groups,
        scratch_shapes=[
            pltpu.VMEM((total, depth), BF16),
            pltpu.VMEM((total, cols), F32),
        ],
        compiler_params=pltpu.CompilerParams(vmem_limit_bytes=24 << 20),
        cost_estimate=pl.CostEstimate(
            flops=2 * total * depth * cols, transcendentals=0, bytes_accessed=2 * depth * cols
        ),
    )(idx, *blocks, w)


def swap_x(x, mask, owners):
    return lax.ppermute(x, "xfer", [(i, i ^ mask) for i in range(owners)])


def shift_z(x, k, groups):
    return lax.ppermute(x, "head", [(i, (i + k) % groups) for i in range(groups)])


def whole(
    kv_pool, lengths, start_device, page_table, queries, new_latent, key_up, value_up, out_proj
):
    owners = lax.axis_size("xfer")
    groups = lax.axis_size("head")
    page_len = kv_pool.shape[1]
    lat_rank = value_up.shape[1]
    heads = key_up.shape[0]
    rows = queries.shape[0]
    idx = jnp.stack([lax.axis_index("xfer"), lax.axis_index("head")])

    other, same = gather_pages(idx, kv_pool, lengths, start_device, page_table, groups)
    part = swap_x(other, 1, owners)
    ring, *sent, side = pack_pages(same, part)
    far = jnp.concatenate([swap_x(x, 2 * m, owners) for m, x in enumerate(sent, 1)], axis=0)
    across = owners - 2
    hops = [(ring, far, swap_x(side, across, owners))]
    for _ in range(groups - 1):
        ring = shift_z(ring, 1, groups)
        far = shift_z(far, 1, groups)
        hops.append((ring, far, swap_x(ring[2:], across, owners)))
    hops = [[(r, 2), (f, f.shape[0]), (s, 2)] for r, f, s in hops]

    q = absorb(queries, key_up)

    dims = (heads, rows, lat_rank, queries.shape[2] ** (-0.5))
    geometry = (owners * groups, groups, lengths.shape[0] // owners, page_len)
    *state, bias = stage(
        idx, q, hops[:1], (0,), dims, geometry, fresh=(lengths, start_device, new_latent)
    )
    end = groups - 1
    for t in range(1, end):
        state = stage(idx, q, [hops[t]], (t,), dims, geometry, state=[bias, *state])
    early, *late = hops[end]
    state = stage(idx, q, [[early]], (end,), dims, geometry, state=[bias, *state])
    head_out = stage(
        idx, q, [late], (end,), dims, geometry, state=[bias, *state],
        value_up=value_up, skips=(2 * page_len,),
    )

    gathered = {}
    for k in range(0, owners, 2):
        gathered[k] = swap_x(head_out, k, owners) if k else head_out
        gathered[k + 1] = swap_x(gathered[k], 1, owners)
    masks = list(range(owners))
    parts = project(idx, masks, [gathered[k] for k in masks], out_proj, groups)
    total = parts[0]
    for k in range(1, groups):
        moved = lax.ppermute(parts[k], "head", [(i, i ^ k) for i in range(groups)])
        total = total + moved.astype(F32)
    return total.astype(BF16)


def solution(mesh):
    in_specs = (
        P(("xfer", "head"), None, None),
        P(),
        P(),
        P(),
        P("xfer", "head", None),
        P("xfer", None),
        P("head", None, None),
        P("head", None, None),
        P("head", "xfer"),
    )
    out_specs = P("head", "xfer")
    return jax.shard_map(whole, mesh=mesh, in_specs=in_specs, out_specs=out_specs, check_vma=False)
```

profile of v0, /device:TPU:0, one launch (start us, length us, event | category | flops | bytes accessed | tf_op | source)
XLA Modules:
  0.0 82.9 jit_solution(10128576187302748552)
XLA Ops:
  0.0 0.1 pad_add_fusion.idx.rest_0_
  0.1 1.8 %shard_map.92 = (bf16[4,64,576]{2,1,0:T(8,128)(2,1)S(1)}, bf16[4,64,576]{2,1,0:T(8,128)(2,1)S(1)}) custom-call(s32[2]{0:T(128)S(1)} %pad_add_fusion.idx.rest_0_, s32[1,64]{1,0:T(1,128)} %bitcast.7, s32[1,64]{1,0:T(1,128)} %bitcast.8, s32[32,64]{1,0:T(8,128)} %bitcast.9, bf16[8,64,576]{2,1,0:T(8,128)(2,1)} %pool_hbm.1), custom_call_target="tpu_custom_call" | custom-call | tf_op jit(solution)/shard_map/pallas_call | solution.py:61
  1.9 0.6 collective-permute-start
  2.4 1.3 %collective-permute-done.part = bf16[4,64,576]{2,1,0:T(8,128)(2,1)S(1)} collective-permute-done((bf16[4,64,576]{2,1,0:T(8,128)(2,1)S(1)}, bf16[4,64,576]{2,1,0:T(8,128)(2,1)S(1)}, u32[]{:S(2)}, u32[]{:S(2)}) %collective-permute-start) | collective-permute-done | bytes 294944 | tf_op jit(solution)/shard_map/ppermute | solution.py:338
  3.7 0.1 shard_map.93
  3.7 2.9 %collective-permute-start.1 = (bf16[2,64,576]{2,1,0:T(8,128)(2,1)S(1)}, bf16[2,64,576]{2,1,0:T(8,128)(2,1)S(1)}, u32[]{:S(2)}, u32[]{:S(2)}) collective-permute-start(bf16[2,64,576]{2,1,0:T(8,128)(2,1)S(1)} %get-tuple-element.31), channel_id=1, source_target_pairs={{0,8},{4,12},{8,0},{12,4},{16,24},{20,28},{24,16},{28,20},{1,9},{5... | collective-permute-start | bytes 442376 | tf_op jit(solution)/shard_map/ppermute | solution.py:338
  6.7 1.5 %collective-permute-start.2 = (bf16[2,64,576]{2,1,0:T(8,128)(2,1)S(1)}, bf16[2,64,576]{2,1,0:T(8,128)(2,1)S(1)}, u32[]{:S(2)}, u32[]{:S(2)}) collective-permute-start(bf16[2,64,576]{2,1,0:T(8,128)(2,1)S(1)} %get-tuple-element.32), channel_id=1, source_target_pairs={{0,16},{4,20},{8,24},{12,28},{16,0},{20,4},{24,8},{28,12},{1,17},{... | collective-permute-start | bytes 442376 | tf_op jit(solution)/shard_map/ppermute | solution.py:338
  8.2 1.6 %collective-permute-start.4 = (bf16[4,64,576]{2,1,0:T(8,128)(2,1)S(1)}, bf16[4,64,576]{2,1,0:T(8,128)(2,1)S(1)}, u32[]{:S(2)}, u32[]{:S(2)}) collective-permute-start(bf16[4,64,576]{2,1,0:T(8,128)(2,1)S(1)} %get-tuple-element.30.rest_5_), channel_id=1, source_target_pairs={{0,1},{1,2},{2,3},{3,0},{4,5},{5,6},{6,7},{7,4},{8,9},{9,10},{10,1... | collective-permute-start | bytes 884744 | tf_op jit(solution)/shard_map/ppermute | solution.py:342
  9.8 1.4 %collective-permute-done.1 = bf16[2,64,576]{2,1,0:T(8,128)(2,1)S(1)} collective-permute-done((bf16[2,64,576]{2,1,0:T(8,128)(2,1)S(1)}, bf16[2,64,576]{2,1,0:T(8,128)(2,1)S(1)}, u32[]{:S(2)}, u32[]{:S(2)}) %collective-permute-start.1) | collective-permute-done | bytes 147488 | tf_op jit(solution)/shard_map/ppermute | solution.py:338
  11.2 1.4 %collective-permute-done.2 = bf16[2,64,576]{2,1,0:T(8,128)(2,1)S(1)} collective-permute-done((bf16[2,64,576]{2,1,0:T(8,128)(2,1)S(1)}, bf16[2,64,576]{2,1,0:T(8,128)(2,1)S(1)}, u32[]{:S(2)}, u32[]{:S(2)}) %collective-permute-start.2) | collective-permute-done | bytes 147488 | tf_op jit(solution)/shard_map/ppermute | solution.py:338
  12.6 1.6 %collective-permute-start.5 = (bf16[4,64,576]{2,1,0:T(8,128)(2,1)S(1)}, bf16[4,64,576]{2,1,0:T(8,128)(2,1)S(1)}, u32[]{:S(2)}, u32[]{:S(2)}) collective-permute-start(bf16[4,64,576]{2,1,0:T(8,128)(2,1)S(1)} %constant_dynamic-update-slice_fusion.rest_6_), channel_id=1, source_target_pairs={{0,1},{1,2},{2,3},{3,0},{4,5},{5,6},{6,7},{7,4},{8,9},{9,10},{10,1... | collective-permute-start | bytes 884744 | tf_op jit(solution)/shard_map/ppermute | solution.py:342
  14.3 6.3 %collective-permute-done.4.rest_6_ = bf16[4,64,576]{2,1,0:T(8,128)(2,1)S(1)} collective-permute-done((bf16[4,64,576]{2,1,0:T(8,128)(2,1)S(1)}, bf16[4,64,576]{2,1,0:T(8,128)(2,1)S(1)}, u32[]{:S(2)}, u32[]{:S(2)}) %collective-permute-start.4) | collective-permute-done | bytes 294944 | tf_op jit(solution)/shard_map/ppermute | solution.py:342
  20.6 0.0 collective-permute-start.7
  20.6 7.0 %collective-permute-done.5.rest_7_ = bf16[4,64,576]{2,1,0:T(8,128)(2,1)S(1)} collective-permute-done((bf16[4,64,576]{2,1,0:T(8,128)(2,1)S(1)}, bf16[4,64,576]{2,1,0:T(8,128)(2,1)S(1)}, u32[]{:S(2)}, u32[]{:S(2)}) %collective-permute-start.5) | collective-permute-done | bytes 294944 | tf_op jit(solution)/shard_map/ppermute | solution.py:342
  27.6 0.0 collective-permute-start.8
  27.6 7.0 %collective-permute-done.7.rest_6_ = bf16[4,64,576]{2,1,0:T(8,128)(2,1)S(1)} collective-permute-done((bf16[4,64,576]{2,1,0:T(8,128)(2,1)S(1)}, bf16[4,64,576]{2,1,0:T(8,128)(2,1)S(1)}, u32[]{:S(2)}, u32[]{:S(2)}) %collective-permute-start.7) | collective-permute-done | bytes 294944 | tf_op jit(solution)/shard_map/ppermute | solution.py:342
  34.6 0.0 collective-permute-start.10
  34.6 0.3 collective-permute-start.3
  34.9 6.8 %collective-permute-done.8.rest_7_ = bf16[4,64,576]{2,1,0:T(8,128)(2,1)S(1)} collective-permute-done((bf16[4,64,576]{2,1,0:T(8,128)(2,1)S(1)}, bf16[4,64,576]{2,1,0:T(8,128)(2,1)S(1)}, u32[]{:S(2)}, u32[]{:S(2)}) %collective-permute-start.8) | collective-permute-done | bytes 294944 | tf_op jit(solution)/shard_map/ppermute | solution.py:342
  41.6 0.0 collective-permute-start.11
  41.6 0.3 collective-permute-start.6
  42.0 2.7 %collective-permute-start.9 = (bf16[2,64,576]{2,1,0:T(8,128)(2,1)S(1)}, bf16[2,64,576]{2,1,0:T(8,128)(2,1)S(1)}, u32[]{:S(2)}, u32[]{:S(2)}) collective-permute-start(bf16[2,64,576]{2,1,0:T(8,128)(2,1)S(1)} %slice.13), channel_id=1, source_target_pairs={{0,24},{4,28},{8,16},{12,20},{16,8},{20,12},{24,0},{28,4},{1,25},{... | collective-permute-start | bytes 442376 | tf_op jit(solution)/shard_map/ppermute | solution.py:338
  44.7 2.6 %shard_map.91.rest_1_ = bf16[512,576]{1,0:T(8,128)(2,1)S(1)} custom-call(bf16[16,32,192]{2,1,0:T(8,128)(2,1)} %queries_hbm.1, bf16[32,128,512]{2,1,0:T(8,128)(2,1)} %key_up_hbm.1), custom_call_target="tpu_custom_call" | custom-call | flops 67108864 | bytes 4194304 | tf_op jit(solution)/shard_map/pallas_call | solution.py:124
  47.3 1.3 %collective-permute-done.10.rest_6_ = bf16[4,64,576]{2,1,0:T(8,128)(2,1)S(1)} collective-permute-done((bf16[4,64,576]{2,1,0:T(8,128)(2,1)S(1)}, bf16[4,64,576]{2,1,0:T(8,128)(2,1)S(1)}, u32[]{:S(2)}, u32[]{:S(2)}) %collective-permute-start.10) | collective-permute-done | bytes 294944 | tf_op jit(solution)/shard_map/ppermute | solution.py:342
  48.7 0.3 collective-permute-start.12
  49.0 0.0 collective-permute-done.3.rest_7_
  49.0 0.0 copy-done.1
  49.0 0.0 copy-done.2
  49.0 0.0 copy-done.3
  49.0 2.9 %shard_map.94 = (f32[512,1]{1,0:T(8,128)S(1)}, f32[512,1]{1,0:T(8,128)S(1)}, f32[512,512]{1,0:T(8,128)S(1)}, f32[4,16,512]{2,1,0:T(8,128)S(1)}) custom-call(s32[2]{0:T(128)S(1)} %pad_add_fusion.idx.rest_0_, bf16[512,576]{1,0:T(8,128)(2,1)S(1)} %shard_map.91.rest_1_, s32[64]{0:T(128)S(1)} %copy-done.1, s32[64]{0:T(128)S(1)} %copy-done.2, ...), custom_call_target="tpu_custom_call" | custom-call | flops 570425344 | bytes 4194304 | tf_op jit(solution)/shard_map/pallas_call | solution.py:286
  51.9 0.0 collective-permute-done.6.rest_8_
  51.9 0.0 copy-start
  52.0 0.0 slice-start
  52.0 2.0 %shard_map.95 = (f32[512,1]{1,0:T(8,128)S(1)}, f32[512,1]{1,0:T(8,128)S(1)}, f32[512,512]{1,0:T(8,128)S(1)}) custom-call(s32[2]{0:T(128)S(1)} %pad_add_fusion.idx.rest_0_, bf16[512,576]{1,0:T(8,128)(2,1)S(1)} %shard_map.91.rest_1_, f32[4,16,512]{2,1,0:T(8,128)S(1)} %get-tuple-element.34.rest_2_, f32[512,1]{1,0:T(8,128)S(1)} %get-tuple-element.35.rest_3_, ...), custom_call_target="tpu_custom_call" | custom-call | flops 570425344 | bytes 4194304 | tf_op jit(solution)/shard_map/pallas_call | solution.py:286
  54.0 0.0 collective-permute-done.9.rest_8_
  54.0 2.0 %shard_map.96 = (f32[512,1]{1,0:T(8,128)S(1)}, f32[512,1]{1,0:T(8,128)S(1)}, f32[512,512]{1,0:T(8,128)S(1)}) custom-call(s32[2]{0:T(128)S(1)} %pad_add_fusion.idx.rest_0_, bf16[512,576]{1,0:T(8,128)(2,1)S(1)} %shard_map.91.rest_1_, f32[4,16,512]{2,1,0:T(8,128)S(1)} %get-tuple-element.34.rest_2_, f32[512,1]{1,0:T(8,128)S(1)} %get-tuple-element.38.rest_3_, ...), custom_call_target="tpu_custom_call" | custom-call | flops 570425344 | bytes 4194304 | tf_op jit(solution)/shard_map/pallas_call | solution.py:286
  56.0 0.0 slice-start.1
  56.0 1.6 %shard_map.97 = (f32[512,1]{1,0:T(8,128)S(1)}, f32[512,1]{1,0:T(8,128)S(1)}, f32[512,512]{1,0:T(8,128)S(1)}) custom-call(s32[2]{0:T(128)S(1)} %pad_add_fusion.idx.rest_0_, bf16[512,576]{1,0:T(8,128)(2,1)S(1)} %shard_map.91.rest_1_, f32[4,16,512]{2,1,0:T(8,128)S(1)} %get-tuple-element.34.rest_2_, f32[512,1]{1,0:T(8,128)S(1)} %get-tuple-element.41.rest_3_, ...), custom_call_target="tpu_custom_call" | custom-call | flops 142606336 | bytes 4194304 | tf_op jit(solution)/shard_map/pallas_call | solution.py:286
  57.7 0.0 collective-permute-done.12.rest_8_
  57.7 0.0 collective-permute-done.11.rest_7_
  57.7 0.0 copy-done
  57.7 3.0 %shard_map.98.rest_0_ = bf16[16,4096]{1,0:T(8,128)(2,1)S(1)} custom-call(s32[2]{0:T(128)S(1)} %pad_add_fusion.idx.rest_0_, bf16[512,576]{1,0:T(8,128)(2,1)S(1)} %shard_map.91.rest_1_, f32[4,16,512]{2,1,0:T(8,128)S(1)} %get-tuple-element.34.rest_2_, f32[512,1]{1,0:T(8,128)S(1)} %get-tuple-element.44.rest_3_, f32[512,1]{1,0:T(8,128)S(1)} %get-tuple-element.45.rest_4_, ...), custom_call_target="tpu_custom_call" | custom-call | flops 427819008 | bytes 4194304 | tf_op jit(solution)/shard_map/pallas_call | solution.py:286
  60.7 1.7 %collective-permute-start.14 = (bf16[16,4096]{1,0:T(8,128)(2,1)S(1)}, bf16[16,4096]{1,0:T(8,128)(2,1)S(1)}, u32[]{:S(2)}, u32[]{:S(2)}) collective-permute-start(bf16[16,4096]{1,0:T(8,128)(2,1)S(1)} %shard_map.98.rest_0_), channel_id=1, source_target_pairs={{0,8},{4,12},{8,0},{12,4},{16,24},{20,28},{24,16},{28,20},{1,9},{5... | collective-permute-start | bytes 393224 | tf_op jit(solution)/shard_map/ppermute | solution.py:338
  62.5 1.5 %collective-permute-start.16 = (bf16[16,4096]{1,0:T(8,128)(2,1)S(1)}, bf16[16,4096]{1,0:T(8,128)(2,1)S(1)}, u32[]{:S(2)}, u32[]{:S(2)}) collective-permute-start(bf16[16,4096]{1,0:T(8,128)(2,1)S(1)} %shard_map.98.rest_0_), channel_id=1, source_target_pairs={{0,16},{4,20},{8,24},{12,28},{16,0},{20,4},{24,8},{28,12},{1,17},{... | collective-permute-start | bytes 393224 | tf_op jit(solution)/shard_map/ppermute | solution.py:338
  64.0 0.3 collective-permute-start.18
  64.2 0.0 collective-permute-start.13
  64.2 1.7 %collective-permute-done.14.rest_2_ = bf16[16,4096]{1,0:T(8,128)(2,1)S(1)} collective-permute-done((bf16[16,4096]{1,0:T(8,128)(2,1)S(1)}, bf16[16,4096]{1,0:T(8,128)(2,1)S(1)}, u32[]{:S(2)}, u32[]{:S(2)}) %collective-permute-start.14) | collective-permute-done | bytes 131104 | tf_op jit(solution)/shard_map/ppermute | solution.py:338
  66.0 0.0 collective-permute-start.15
  66.0 1.4 %collective-permute-done.16.rest_4_ = bf16[16,4096]{1,0:T(8,128)(2,1)S(1)} collective-permute-done((bf16[16,4096]{1,0:T(8,128)(2,1)S(1)}, bf16[16,4096]{1,0:T(8,128)(2,1)S(1)}, u32[]{:S(2)}, u32[]{:S(2)}) %collective-permute-start.16) | collective-permute-done | bytes 131104 | tf_op jit(solution)/shard_map/ppermute | solution.py:338
  67.4 0.0 collective-permute-start.17
  67.4 2.4 %collective-permute-done.18.rest_6_ = bf16[16,4096]{1,0:T(8,128)(2,1)S(1)} collective-permute-done((bf16[16,4096]{1,0:T(8,128)(2,1)S(1)}, bf16[16,4096]{1,0:T(8,128)(2,1)S(1)}, u32[]{:S(2)}, u32[]{:S(2)}) %collective-permute-start.18) | collective-permute-done | bytes 131104 | tf_op jit(solution)/shard_map/ppermute | solution.py:338
  69.8 0.0 collective-permute-start.19
  69.8 0.0 collective-permute-done.13.rest_1_
  69.8 0.0 collective-permute-done.15.rest_3_
  69.8 0.0 collective-permute-done.17.rest_5_
  69.9 1.3 %collective-permute-done.19.rest_7_ = bf16[16,4096]{1,0:T(8,128)(2,1)S(1)} collective-permute-done((bf16[16,4096]{1,0:T(8,128)(2,1)S(1)}, bf16[16,4096]{1,0:T(8,128)(2,1)S(1)}, u32[]{:S(2)}, u32[]{:S(2)}) %collective-permute-start.19) | collective-permute-done | bytes 131104 | tf_op jit(solution)/shard_map/ppermute | solution.py:338
  71.2 1.9 %shard_map.99 = (f32[32,896]{1,0:T(8,128)S(1)}, bf16[32,896]{1,0:T(8,128)(2,1)S(1)}, bf16[32,896]{1,0:T(8,128)(2,1)S(1)}, bf16[32,896]{1,0:T(8,128)(2,1)S(1)}) custom-call(s32[2]{0:T(128)S(1)} %pad_add_fusion.idx.rest_0_, bf16[16,4096]{1,0:T(8,128)(2,1)S(1)} %shard_map.98.rest_0_, bf16[16,4096]{1,0:T(8,128)(2,1)S(1)} %collective-permute-done.13.rest_1_, ...), custom_call_target="tpu_custom_call" | custom-call | flops 939524096 | bytes 7340032 | tf_op jit(solution)/shard_map/pallas_call | solution.py:321
  73.1 0.1 collective-permute-start.20
  73.2 3.1 %collective-permute-start.21 = (bf16[32,896]{1,0:T(8,128)(2,1)S(1)}, bf16[32,896]{1,0:T(8,128)(2,1)S(1)}, u32[]{:S(2)}, u32[]{:S(2)}) collective-permute-start(bf16[32,896]{1,0:T(8,128)(2,1)S(1)} %get-tuple-element.49), channel_id=1, source_target_pairs={{0,2},{1,3},{2,0},{3,1},{4,6},{5,7},{6,4},{7,5},{8,10},{9,11},{10,... | collective-permute-start | bytes 172040 | tf_op jit(solution)/shard_map/ppermute | solution.py:393
  76.3 1.3 %collective-permute-start.22 = (bf16[32,896]{1,0:T(8,128)(2,1)S(1)}, bf16[32,896]{1,0:T(8,128)(2,1)S(1)}, u32[]{:S(2)}, u32[]{:S(2)}) collective-permute-start(bf16[32,896]{1,0:T(8,128)(2,1)S(1)} %get-tuple-element.50), channel_id=1, source_target_pairs={{0,3},{1,2},{2,1},{3,0},{4,7},{5,6},{6,5},{7,4},{8,11},{9,10},{10,... | collective-permute-start | bytes 172040 | tf_op jit(solution)/shard_map/ppermute | solution.py:393
  77.6 0.7 collective-permute-done.20
  78.2 1.8 %collective-permute-done.21 = bf16[32,896]{1,0:T(8,128)(2,1)S(1)} collective-permute-done((bf16[32,896]{1,0:T(8,128)(2,1)S(1)}, bf16[32,896]{1,0:T(8,128)(2,1)S(1)}, u32[]{:S(2)}, u32[]{:S(2)}) %collective-permute-start.21) | collective-permute-done | bytes 57376 | tf_op jit(solution)/shard_map/ppermute | solution.py:393
  80.0 2.3 %collective-permute-done.22 = bf16[32,896]{1,0:T(8,128)(2,1)S(1)} collective-permute-done((bf16[32,896]{1,0:T(8,128)(2,1)S(1)}, bf16[32,896]{1,0:T(8,128)(2,1)S(1)}, u32[]{:S(2)}, u32[]{:S(2)}) %collective-permute-start.22) | collective-permute-done | bytes 57376 | tf_op jit(solution)/shard_map/ppermute | solution.py:393
  82.3 0.7 add_convert_fusion
  (11 shorter events, 0.1 us)
Async XLA Ops:
  0.0 49.0 %copy-start.1 = (s32[64]{0:T(128)S(1)}, s32[64]{0:T(128)}, u32[]{:S(2)}) copy-start(s32[64]{0:T(128)} %rest_2_.1) | copy-start | bytes 772
  0.0 49.0 %copy-start.2 = (s32[64]{0:T(128)S(1)}, s32[64]{0:T(128)}, u32[]{:S(2)}) copy-start(s32[64]{0:T(128)} %rest_3_.1) | copy-start | bytes 772
  0.0 49.0 %copy-start.3 = (bf16[16,576]{1,0:T(8,128)(2,1)S(1)}, bf16[16,576]{1,0:T(8,128)(2,1)}, u32[]{:S(2)}) copy-start(bf16[16,576]{1,0:T(8,128)(2,1)} %rest_4_.1) | copy-start | bytes 55300
  1.9 1.8 %collective-permute-start = (bf16[4,64,576]{2,1,0:T(8,128)(2,1)S(1)}, bf16[4,64,576]{2,1,0:T(8,128)(2,1)S(1)}, u32[]{:S(2)}, u32[]{:S(2)}) collective-permute-start(bf16[4,64,576]{2,1,0:T(8,128)(2,1)S(1)} %get-tuple-element.29), channel_id=1, source_target_pairs={{0,4},{4,0},{8,12},{12,8},{16,20},{20,16},{24,28},{28,24},{1,5},{5... | collective-permute-start | bytes 884744 | tf_op jit(solution)/shard_map/ppermute | solution.py:338
  3.7 7.4 %collective-permute-start.1 = (bf16[2,64,576]{2,1,0:T(8,128)(2,1)S(1)}, bf16[2,64,576]{2,1,0:T(8,128)(2,1)S(1)}, u32[]{:S(2)}, u32[]{:S(2)}) collective-permute-start(bf16[2,64,576]{2,1,0:T(8,128)(2,1)S(1)} %get-tuple-element.31), channel_id=1, source_target_pairs={{0,8},{4,12},{8,0},{12,4},{16,24},{20,28},{24,16},{28,20},{1,9},{5... | collective-permute-start | bytes 442376 | tf_op jit(solution)/shard_map/ppermute | solution.py:338
  6.7 6.0 %collective-permute-start.2 = (bf16[2,64,576]{2,1,0:T(8,128)(2,1)S(1)}, bf16[2,64,576]{2,1,0:T(8,128)(2,1)S(1)}, u32[]{:S(2)}, u32[]{:S(2)}) collective-permute-start(bf16[2,64,576]{2,1,0:T(8,128)(2,1)S(1)} %get-tuple-element.32), channel_id=1, source_target_pairs={{0,16},{4,20},{8,24},{12,28},{16,0},{20,4},{24,8},{28,12},{1,17},{... | collective-permute-start | bytes 442376 | tf_op jit(solution)/shard_map/ppermute | solution.py:338
  8.2 12.4 %collective-permute-start.4 = (bf16[4,64,576]{2,1,0:T(8,128)(2,1)S(1)}, bf16[4,64,576]{2,1,0:T(8,128)(2,1)S(1)}, u32[]{:S(2)}, u32[]{:S(2)}) collective-permute-start(bf16[4,64,576]{2,1,0:T(8,128)(2,1)S(1)} %get-tuple-element.30.rest_5_), channel_id=1, source_target_pairs={{0,1},{1,2},{2,3},{3,0},{4,5},{5,6},{6,7},{7,4},{8,9},{9,10},{10,1... | collective-permute-start | bytes 884744 | tf_op jit(solution)/shard_map/ppermute | solution.py:342
  12.6 14.9 %collective-permute-start.5 = (bf16[4,64,576]{2,1,0:T(8,128)(2,1)S(1)}, bf16[4,64,576]{2,1,0:T(8,128)(2,1)S(1)}, u32[]{:S(2)}, u32[]{:S(2)}) collective-permute-start(bf16[4,64,576]{2,1,0:T(8,128)(2,1)S(1)} %constant_dynamic-update-slice_fusion.rest_6_), channel_id=1, source_target_pairs={{0,1},{1,2},{2,3},{3,0},{4,5},{5,6},{6,7},{7,4},{8,9},{9,10},{10,1... | collective-permute-start | bytes 884744 | tf_op jit(solution)/shard_map/ppermute | solution.py:342
  20.6 14.0 %collective-permute-start.7 = (bf16[4,64,576]{2,1,0:T(8,128)(2,1)S(1)}, bf16[4,64,576]{2,1,0:T(8,128)(2,1)S(1)}, u32[]{:S(2)}, u32[]{:S(2)}) collective-permute-start(bf16[4,64,576]{2,1,0:T(8,128)(2,1)S(1)} %collective-permute-done.4.rest_6_), channel_id=1, source_target_pairs={{0,1},{1,2},{2,3},{3,0},{4,5},{5,6},{6,7},{7,4},{8,9},{9,10},{10,1... | collective-permute-start | bytes 884744 | tf_op jit(solution)/shard_map/ppermute | solution.py:342
  27.6 14.0 %collective-permute-start.8 = (bf16[4,64,576]{2,1,0:T(8,128)(2,1)S(1)}, bf16[4,64,576]{2,1,0:T(8,128)(2,1)S(1)}, u32[]{:S(2)}, u32[]{:S(2)}) collective-permute-start(bf16[4,64,576]{2,1,0:T(8,128)(2,1)S(1)} %collective-permute-done.5.rest_7_), channel_id=1, source_target_pairs={{0,1},{1,2},{2,3},{3,0},{4,5},{5,6},{6,7},{7,4},{8,9},{9,10},{10,1... | collective-permute-start | bytes 884744 | tf_op jit(solution)/shard_map/ppermute | solution.py:342
  34.6 14.0 %collective-permute-start.10 = (bf16[4,64,576]{2,1,0:T(8,128)(2,1)S(1)}, bf16[4,64,576]{2,1,0:T(8,128)(2,1)S(1)}, u32[]{:S(2)}, u32[]{:S(2)}) collective-permute-start(bf16[4,64,576]{2,1,0:T(8,128)(2,1)S(1)} %collective-permute-done.7.rest_6_), channel_id=1, source_target_pairs={{0,1},{1,2},{2,3},{3,0},{4,5},{5,6},{6,7},{7,4},{8,9},{9,10},{10,1... | collective-permute-start | bytes 884744 | tf_op jit(solution)/shard_map/ppermute | solution.py:342
  34.6 14.4 %collective-permute-start.3 = (bf16[2,64,576]{2,1,0:T(8,128)(2,1)S(1)}, bf16[2,64,576]{2,1,0:T(8,128)(2,1)S(1)}, u32[]{:S(2)}, u32[]{:S(2)}) collective-permute-start(bf16[2,64,576]{2,1,0:T(8,128)(2,1)S(1)} %get-tuple-element.33), channel_id=1, source_target_pairs={{0,24},{4,28},{8,16},{12,20},{16,8},{20,12},{24,0},{28,4},{1,25},{... | collective-permute-start | bytes 442376 | tf_op jit(solution)/shard_map/ppermute | solution.py:338
  41.6 16.0 %collective-permute-start.11 = (bf16[4,64,576]{2,1,0:T(8,128)(2,1)S(1)}, bf16[4,64,576]{2,1,0:T(8,128)(2,1)S(1)}, u32[]{:S(2)}, u32[]{:S(2)}) collective-permute-start(bf16[4,64,576]{2,1,0:T(8,128)(2,1)S(1)} %collective-permute-done.8.rest_7_), channel_id=1, source_target_pairs={{0,1},{1,2},{2,3},{3,0},{4,5},{5,6},{6,7},{7,4},{8,9},{9,10},{10,1... | collective-permute-start | bytes 884744 | tf_op jit(solution)/shard_map/ppermute | solution.py:342
  41.6 10.3 %collective-permute-start.6 = (bf16[2,64,576]{2,1,0:T(8,128)(2,1)S(1)}, bf16[2,64,576]{2,1,0:T(8,128)(2,1)S(1)}, u32[]{:S(2)}, u32[]{:S(2)}) collective-permute-start(bf16[2,64,576]{2,1,0:T(8,128)(2,1)S(1)} %slice.12), channel_id=1, source_target_pairs={{0,24},{4,28},{8,16},{12,20},{16,8},{20,12},{24,0},{28,4},{1,25},{... | collective-permute-start | bytes 442376 | tf_op jit(solution)/shard_map/ppermute | solution.py:338
  42.0 12.0 %collective-permute-start.9 = (bf16[2,64,576]{2,1,0:T(8,128)(2,1)S(1)}, bf16[2,64,576]{2,1,0:T(8,128)(2,1)S(1)}, u32[]{:S(2)}, u32[]{:S(2)}) collective-permute-start(bf16[2,64,576]{2,1,0:T(8,128)(2,1)S(1)} %slice.13), channel_id=1, source_target_pairs={{0,24},{4,28},{8,16},{12,20},{16,8},{20,12},{24,0},{28,4},{1,25},{... | collective-permute-start | bytes 442376 | tf_op jit(solution)/shard_map/ppermute | solution.py:338
  48.7 9.0 %collective-permute-start.12 = (bf16[2,64,576]{2,1,0:T(8,128)(2,1)S(1)}, bf16[2,64,576]{2,1,0:T(8,128)(2,1)S(1)}, u32[]{:S(2)}, u32[]{:S(2)}) collective-permute-start(bf16[2,64,576]{2,1,0:T(8,128)(2,1)S(1)} %slice.14), channel_id=1, source_target_pairs={{0,24},{4,28},{8,16},{12,20},{16,8},{20,12},{24,0},{28,4},{1,25},{... | collective-permute-start | bytes 442376 | tf_op jit(solution)/shard_map/ppermute | solution.py:338
  51.9 5.7 %copy-start = (bf16[32,512,128]{2,1,0:T(8,128)(2,1)S(1)}, bf16[32,512,128]{2,1,0:T(8,128)(2,1)}, u32[]{:S(2)}) copy-start(bf16[32,512,128]{2,1,0:T(8,128)(2,1)} %rest_6_.1) | copy-start | bytes 12582916
  52.0 19.2 %slice-start = ((s8[7340032]{0:T(1024)(128)(4,1)}), s8[4194304]{0:T(1024)(128)(4,1)S(1)}, s32[]{:S(2)}) async-start(s8[7340032]{0:T(1024)(128)(4,1)} %bitcast.5), calls=%async_computation | async-start | bytes 8388608
  56.0 15.2 %slice-start.1 = ((s8[7340032]{0:T(1024)(128)(4,1)}), s8[3145728]{0:T(1024)(128)(4,1)S(1)}, s32[]{:S(2)}) async-start(s8[7340032]{0:T(1024)(128)(4,1)} %bitcast.5), calls=%async_computation.1 | async-start | bytes 6291456
  60.7 5.3 %collective-permute-start.14 = (bf16[16,4096]{1,0:T(8,128)(2,1)S(1)}, bf16[16,4096]{1,0:T(8,128)(2,1)S(1)}, u32[]{:S(2)}, u32[]{:S(2)}) collective-permute-start(bf16[16,4096]{1,0:T(8,128)(2,1)S(1)} %shard_map.98.rest_0_), channel_id=1, source_target_pairs={{0,8},{4,12},{8,0},{12,4},{16,24},{20,28},{24,16},{28,20},{1,9},{5... | collective-permute-start | bytes 393224 | tf_op jit(solution)/shard_map/ppermute | solution.py:338
  62.5 5.0 %collective-permute-start.16 = (bf16[16,4096]{1,0:T(8,128)(2,1)S(1)}, bf16[16,4096]{1,0:T(8,128)(2,1)S(1)}, u32[]{:S(2)}, u32[]{:S(2)}) collective-permute-start(bf16[16,4096]{1,0:T(8,128)(2,1)S(1)} %shard_map.98.rest_0_), channel_id=1, source_target_pairs={{0,16},{4,20},{8,24},{12,28},{16,0},{20,4},{24,8},{28,12},{1,17},{... | collective-permute-start | bytes 393224 | tf_op jit(solution)/shard_map/ppermute | solution.py:338
  64.0 5.9 %collective-permute-start.18 = (bf16[16,4096]{1,0:T(8,128)(2,1)S(1)}, bf16[16,4096]{1,0:T(8,128)(2,1)S(1)}, u32[]{:S(2)}, u32[]{:S(2)}) collective-permute-start(bf16[16,4096]{1,0:T(8,128)(2,1)S(1)} %shard_map.98.rest_0_), channel_id=1, source_target_pairs={{0,24},{4,28},{8,16},{12,20},{16,8},{20,12},{24,0},{28,4},{1,25},{... | collective-permute-start | bytes 393224 | tf_op jit(solution)/shard_map/ppermute | solution.py:338
  64.2 5.6 %collective-permute-start.13 = (bf16[16,4096]{1,0:T(8,128)(2,1)S(1)}, bf16[16,4096]{1,0:T(8,128)(2,1)S(1)}, u32[]{:S(2)}, u32[]{:S(2)}) collective-permute-start(bf16[16,4096]{1,0:T(8,128)(2,1)S(1)} %shard_map.98.rest_0_), channel_id=1, source_target_pairs={{0,4},{4,0},{8,12},{12,8},{16,20},{20,16},{24,28},{28,24},{1,5},{5... | collective-permute-start | bytes 393224 | tf_op jit(solution)/shard_map/ppermute | solution.py:338
  66.0 3.9 %collective-permute-start.15 = (bf16[16,4096]{1,0:T(8,128)(2,1)S(1)}, bf16[16,4096]{1,0:T(8,128)(2,1)S(1)}, u32[]{:S(2)}, u32[]{:S(2)}) collective-permute-start(bf16[16,4096]{1,0:T(8,128)(2,1)S(1)} %collective-permute-done.14.rest_2_), channel_id=1, source_target_pairs={{0,4},{4,0},{8,12},{12,8},{16,20},{20,16},{24,28},{28,24},{1,5},{5... | collective-permute-start | bytes 393224 | tf_op jit(solution)/shard_map/ppermute | solution.py:338
  67.4 2.4 %collective-permute-start.17 = (bf16[16,4096]{1,0:T(8,128)(2,1)S(1)}, bf16[16,4096]{1,0:T(8,128)(2,1)S(1)}, u32[]{:S(2)}, u32[]{:S(2)}) collective-permute-start(bf16[16,4096]{1,0:T(8,128)(2,1)S(1)} %collective-permute-done.16.rest_4_), channel_id=1, source_target_pairs={{0,4},{4,0},{8,12},{12,8},{16,20},{20,16},{24,28},{28,24},{1,5},{5... | collective-permute-start | bytes 393224 | tf_op jit(solution)/shard_map/ppermute | solution.py:338
  69.8 1.3 %collective-permute-start.19 = (bf16[16,4096]{1,0:T(8,128)(2,1)S(1)}, bf16[16,4096]{1,0:T(8,128)(2,1)S(1)}, u32[]{:S(2)}, u32[]{:S(2)}) collective-permute-start(bf16[16,4096]{1,0:T(8,128)(2,1)S(1)} %collective-permute-done.18.rest_6_), channel_id=1, source_target_pairs={{0,4},{4,0},{8,12},{12,8},{16,20},{20,16},{24,28},{28,24},{1,5},{5... | collective-permute-start | bytes 393224 | tf_op jit(solution)/shard_map/ppermute | solution.py:338
  73.1 5.1 %collective-permute-start.20 = (bf16[32,896]{1,0:T(8,128)(2,1)S(1)}, bf16[32,896]{1,0:T(8,128)(2,1)S(1)}, u32[]{:S(2)}, u32[]{:S(2)}) collective-permute-start(bf16[32,896]{1,0:T(8,128)(2,1)S(1)} %get-tuple-element.48), channel_id=1, source_target_pairs={{0,1},{1,0},{2,3},{3,2},{4,5},{5,4},{6,7},{7,6},{8,9},{9,8},{10,11... | collective-permute-start | bytes 172040 | tf_op jit(solution)/shard_map/ppermute | solution.py:393
  73.2 6.8 %collective-permute-start.21 = (bf16[32,896]{1,0:T(8,128)(2,1)S(1)}, bf16[32,896]{1,0:T(8,128)(2,1)S(1)}, u32[]{:S(2)}, u32[]{:S(2)}) collective-permute-start(bf16[32,896]{1,0:T(8,128)(2,1)S(1)} %get-tuple-element.49), channel_id=1, source_target_pairs={{0,2},{1,3},{2,0},{3,1},{4,6},{5,7},{6,4},{7,5},{8,10},{9,11},{10,... | collective-permute-start | bytes 172040 | tf_op jit(solution)/shard_map/ppermute | solution.py:393
  76.3 6.0 %collective-permute-start.22 = (bf16[32,896]{1,0:T(8,128)(2,1)S(1)}, bf16[32,896]{1,0:T(8,128)(2,1)S(1)}, u32[]{:S(2)}, u32[]{:S(2)}) collective-permute-start(bf16[32,896]{1,0:T(8,128)(2,1)S(1)} %get-tuple-element.50), channel_id=1, source_target_pairs={{0,3},{1,2},{2,1},{3,0},{4,7},{5,6},{6,5},{7,4},{8,11},{9,10},{10,... | collective-permute-start | bytes 172040 | tf_op jit(solution)/shard_map/ppermute | solution.py:393
where the time goes:
time: 83.1 us; the launch traced here: 82.9 us
  waiting for transfers between devices  44.1 us (53%)
  starting transfers between devices  19.8 us (24%)
  Pallas kernels  17.9 us (22%)
    ppermute x6, waiting for transfers between devices, shift_z(): lax.ppermute(x, 'head', [(i, (i + k) % groups) for i in range(groups)])  28.4 us
    ppermute x14, starting transfers between devices, swap_x(): return lax.ppermute(x, 'xfer', [(i, i ^ mask) for i in range(owners)])  12.2 us
    pallas_call x5, Pallas kernels, stage(): pl.pallas_call(functools.partial(stage_kernel, cfg), out_shape=out_shape,...  11.6 us
    ppermute x14, waiting for transfers between devices, swap_x(): return lax.ppermute(x, 'xfer', [(i, i ^ mask) for i in range(owners)])  11 us
    ppermute x3, waiting for transfers between devices, whole(): moved = lax.ppermute(parts[k], 'head', [(i, i ^ k) for i in range(groups)])  4.69 us
    ppermute x3, starting transfers between devices, whole(): moved = lax.ppermute(parts[k], 'head', [(i, i ^ k) for i in range(groups)])  4.45 us
    ppermute x6, starting transfers between devices, shift_z(): lax.ppermute(x, 'head', [(i, (i + k) % groups) for i in range(groups)])  3.22 us
    pallas_call x1, Pallas kernels, absorb(): pl.pallas_call(absorb_kernel, out_shape=jax.ShapeDtypeStruct((heads * row...  2.59 us
  transfers between devices with their start and end apart: 23, of which 15 were waited for; matrix products, arithmetic and copies ran while one was open for 0% of the time, Pallas kernels for 13%

commit v1 on v0

--- a/solution.py
+++ b/solution.py
@@ -140,8 +140,8 @@
     )(*args)
 
 
-def row_chunks(heads, rows):
-    size = max(1, 512 // rows)
+def row_chunks(heads, rows, most):
+    size = max(1, most // rows)
     return [(h, min(size, heads - h)) for h in range(0, heads, size)]
 
 
@@ -232,7 +232,7 @@
             n = pages * ref.shape[1]
             parts.append((ref[:pages].reshape(n, -1), bias[plane, :, at : at + n]))
             at += n
-    for h, n in row_chunks(heads, rows):
+    for h, n in row_chunks(heads, rows, 256 if last else 512):
         at = pl.ds(h * rows, n * rows)
         old = None if first else (m_in[at], l_in[at], acc_in[at])
         m, l, acc = attend(q[at], parts, scale, lat_rank, old)

time: 83.1 us -> 83 us (level)
  no operation moved by 1% of the time
where the time goes in v1:
time: 83 us; the launch traced here: 82.8 us
  waiting for transfers between devices  44.1 us (53%)
  starting transfers between devices  19.8 us (24%)
  Pallas kernels  17.8 us (21%)
    ppermute x6, waiting for transfers between devices, shift_z(): lax.ppermute(x, 'head', [(i, (i + k) % groups) for i in range(groups)])  28.4 us
    ppermute x14, starting transfers between devices, swap_x(): return lax.ppermute(x, 'xfer', [(i, i ^ mask) for i in range(owners)])  12.2 us
    pallas_call x5, Pallas kernels, stage(): pl.pallas_call(functools.partial(stage_kernel, cfg), out_shape=out_shape,...  11.5 us
    ppermute x14, waiting for transfers between devices, swap_x(): return lax.ppermute(x, 'xfer', [(i, i ^ mask) for i in range(owners)])  11 us
    ppermute x3, waiting for transfers between devices, whole(): moved = lax.ppermute(parts[k], 'head', [(i, i ^ k) for i in range(groups)])  4.69 us
    ppermute x3, starting transfers between devices, whole(): moved = lax.ppermute(parts[k], 'head', [(i, i ^ k) for i in range(groups)])  4.45 us
    ppermute x6, starting transfers between devices, shift_z(): lax.ppermute(x, 'head', [(i, (i + k) % groups) for i in range(groups)])  3.22 us
    pallas_call x1, Pallas kernels, absorb(): pl.pallas_call(absorb_kernel, out_shape=jax.ShapeDtypeStruct((heads * row...  2.59 us
  transfers between devices with their start and end apart: 23, of which 15 were waited for; matrix products, arithmetic and copies ran while one was open for 0% of the time, Pallas kernels for 13%

profile of v1, /device:TPU:0, one launch (start us, length us, event | category | flops | bytes accessed | tf_op | source)
XLA Modules:
  0.0 82.8 jit_solution(9223707382523357760)
XLA Ops:
  0.0 0.1 pad_add_fusion.idx.rest_0_
  0.1 1.8 %shard_map.92 = (bf16[4,64,576]{2,1,0:T(8,128)(2,1)S(1)}, bf16[4,64,576]{2,1,0:T(8,128)(2,1)S(1)}) custom-call(s32[2]{0:T(128)S(1)} %pad_add_fusion.idx.rest_0_, s32[1,64]{1,0:T(1,128)} %bitcast.7, s32[1,64]{1,0:T(1,128)} %bitcast.8, s32[32,64]{1,0:T(8,128)} %bitcast.9, bf16[8,64,576]{2,1,0:T(8,128)(2,1)} %pool_hbm.1), custom_call_target="tpu_custom_call" | custom-call | tf_op jit(solution)/shard_map/pallas_call | solution.py:61
  1.9 0.6 collective-permute-start
  2.4 1.3 %collective-permute-done.part = bf16[4,64,576]{2,1,0:T(8,128)(2,1)S(1)} collective-permute-done((bf16[4,64,576]{2,1,0:T(8,128)(2,1)S(1)}, bf16[4,64,576]{2,1,0:T(8,128)(2,1)S(1)}, u32[]{:S(2)}, u32[]{:S(2)}) %collective-permute-start) | collective-permute-done | bytes 294944 | tf_op jit(solution)/shard_map/ppermute | solution.py:338
  3.7 0.1 shard_map.93
  3.7 2.9 %collective-permute-start.1 = (bf16[2,64,576]{2,1,0:T(8,128)(2,1)S(1)}, bf16[2,64,576]{2,1,0:T(8,128)(2,1)S(1)}, u32[]{:S(2)}, u32[]{:S(2)}) collective-permute-start(bf16[2,64,576]{2,1,0:T(8,128)(2,1)S(1)} %get-tuple-element.31), channel_id=1, source_target_pairs={{0,8},{4,12},{8,0},{12,4},{16,24},{20,28},{24,16},{28,20},{1,9},{5... | collective-permute-start | bytes 442376 | tf_op jit(solution)/shard_map/ppermute | solution.py:338
  6.7 1.5 %collective-permute-start.2 = (bf16[2,64,576]{2,1,0:T(8,128)(2,1)S(1)}, bf16[2,64,576]{2,1,0:T(8,128)(2,1)S(1)}, u32[]{:S(2)}, u32[]{:S(2)}) collective-permute-start(bf16[2,64,576]{2,1,0:T(8,128)(2,1)S(1)} %get-tuple-element.32), channel_id=1, source_target_pairs={{0,16},{4,20},{8,24},{12,28},{16,0},{20,4},{24,8},{28,12},{1,17},{... | collective-permute-start | bytes 442376 | tf_op jit(solution)/shard_map/ppermute | solution.py:338
  8.2 1.6 %collective-permute-start.4 = (bf16[4,64,576]{2,1,0:T(8,128)(2,1)S(1)}, bf16[4,64,576]{2,1,0:T(8,128)(2,1)S(1)}, u32[]{:S(2)}, u32[]{:S(2)}) collective-permute-start(bf16[4,64,576]{2,1,0:T(8,128)(2,1)S(1)} %get-tuple-element.30.rest_5_), channel_id=1, source_target_pairs={{0,1},{1,2},{2,3},{3,0},{4,5},{5,6},{6,7},{7,4},{8,9},{9,10},{10,1... | collective-permute-start | bytes 884744 | tf_op jit(solution)/shard_map/ppermute | solution.py:342
  9.8 1.4 %collective-permute-done.1 = bf16[2,64,576]{2,1,0:T(8,128)(2,1)S(1)} collective-permute-done((bf16[2,64,576]{2,1,0:T(8,128)(2,1)S(1)}, bf16[2,64,576]{2,1,0:T(8,128)(2,1)S(1)}, u32[]{:S(2)}, u32[]{:S(2)}) %collective-permute-start.1) | collective-permute-done | bytes 147488 | tf_op jit(solution)/shard_map/ppermute | solution.py:338
  11.2 1.4 %collective-permute-done.2 = bf16[2,64,576]{2,1,0:T(8,128)(2,1)S(1)} collective-permute-done((bf16[2,64,576]{2,1,0:T(8,128)(2,1)S(1)}, bf16[2,64,576]{2,1,0:T(8,128)(2,1)S(1)}, u32[]{:S(2)}, u32[]{:S(2)}) %collective-permute-start.2) | collective-permute-done | bytes 147488 | tf_op jit(solution)/shard_map/ppermute | solution.py:338
  12.6 1.6 %collective-permute-start.5 = (bf16[4,64,576]{2,1,0:T(8,128)(2,1)S(1)}, bf16[4,64,576]{2,1,0:T(8,128)(2,1)S(1)}, u32[]{:S(2)}, u32[]{:S(2)}) collective-permute-start(bf16[4,64,576]{2,1,0:T(8,128)(2,1)S(1)} %constant_dynamic-update-slice_fusion.rest_6_), channel_id=1, source_target_pairs={{0,1},{1,2},{2,3},{3,0},{4,5},{5,6},{6,7},{7,4},{8,9},{9,10},{10,1... | collective-permute-start | bytes 884744 | tf_op jit(solution)/shard_map/ppermute | solution.py:342
  14.3 6.3 %collective-permute-done.4.rest_6_ = bf16[4,64,576]{2,1,0:T(8,128)(2,1)S(1)} collective-permute-done((bf16[4,64,576]{2,1,0:T(8,128)(2,1)S(1)}, bf16[4,64,576]{2,1,0:T(8,128)(2,1)S(1)}, u32[]{:S(2)}, u32[]{:S(2)}) %collective-permute-start.4) | collective-permute-done | bytes 294944 | tf_op jit(solution)/shard_map/ppermute | solution.py:342
  20.6 0.0 collective-permute-start.7
  20.6 7.0 %collective-permute-done.5.rest_7_ = bf16[4,64,576]{2,1,0:T(8,128)(2,1)S(1)} collective-permute-done((bf16[4,64,576]{2,1,0:T(8,128)(2,1)S(1)}, bf16[4,64,576]{2,1,0:T(8,128)(2,1)S(1)}, u32[]{:S(2)}, u32[]{:S(2)}) %collective-permute-start.5) | collective-permute-done | bytes 294944 | tf_op jit(solution)/shard_map/ppermute | solution.py:342
  27.6 0.0 collective-permute-start.8
  27.6 7.0 %collective-permute-done.7.rest_6_ = bf16[4,64,576]{2,1,0:T(8,128)(2,1)S(1)} collective-permute-done((bf16[4,64,576]{2,1,0:T(8,128)(2,1)S(1)}, bf16[4,64,576]{2,1,0:T(8,128)(2,1)S(1)}, u32[]{:S(2)}, u32[]{:S(2)}) %collective-permute-start.7) | collective-permute-done | bytes 294944 | tf_op jit(solution)/shard_map/ppermute | solution.py:342
  34.6 0.0 collective-permute-start.10
  34.6 0.3 collective-permute-start.3
  34.9 6.8 %collective-permute-done.8.rest_7_ = bf16[4,64,576]{2,1,0:T(8,128)(2,1)S(1)} collective-permute-done((bf16[4,64,576]{2,1,0:T(8,128)(2,1)S(1)}, bf16[4,64,576]{2,1,0:T(8,128)(2,1)S(1)}, u32[]{:S(2)}, u32[]{:S(2)}) %collective-permute-start.8) | collective-permute-done | bytes 294944 | tf_op jit(solution)/shard_map/ppermute | solution.py:342
  41.6 0.0 collective-permute-start.11
  41.6 0.3 collective-permute-start.6
  42.0 2.7 %collective-permute-start.9 = (bf16[2,64,576]{2,1,0:T(8,128)(2,1)S(1)}, bf16[2,64,576]{2,1,0:T(8,128)(2,1)S(1)}, u32[]{:S(2)}, u32[]{:S(2)}) collective-permute-start(bf16[2,64,576]{2,1,0:T(8,128)(2,1)S(1)} %slice.13), channel_id=1, source_target_pairs={{0,24},{4,28},{8,16},{12,20},{16,8},{20,12},{24,0},{28,4},{1,25},{... | collective-permute-start | bytes 442376 | tf_op jit(solution)/shard_map/ppermute | solution.py:338
  44.7 2.6 %shard_map.91.rest_1_ = bf16[512,576]{1,0:T(8,128)(2,1)S(1)} custom-call(bf16[16,32,192]{2,1,0:T(8,128)(2,1)} %queries_hbm.1, bf16[32,128,512]{2,1,0:T(8,128)(2,1)} %key_up_hbm.1), custom_call_target="tpu_custom_call" | custom-call | flops 67108864 | bytes 4194304 | tf_op jit(solution)/shard_map/pallas_call | solution.py:124
  47.3 1.3 %collective-permute-done.10.rest_6_ = bf16[4,64,576]{2,1,0:T(8,128)(2,1)S(1)} collective-permute-done((bf16[4,64,576]{2,1,0:T(8,128)(2,1)S(1)}, bf16[4,64,576]{2,1,0:T(8,128)(2,1)S(1)}, u32[]{:S(2)}, u32[]{:S(2)}) %collective-permute-start.10) | collective-permute-done | bytes 294944 | tf_op jit(solution)/shard_map/ppermute | solution.py:342
  48.7 0.3 collective-permute-start.12
  49.0 0.0 collective-permute-done.3.rest_7_
  49.0 0.0 copy-done.1
  49.0 0.0 copy-done.2
  49.0 0.0 copy-done.3
  49.0 2.9 %shard_map.94 = (f32[512,1]{1,0:T(8,128)S(1)}, f32[512,1]{1,0:T(8,128)S(1)}, f32[512,512]{1,0:T(8,128)S(1)}, f32[4,16,512]{2,1,0:T(8,128)S(1)}) custom-call(s32[2]{0:T(128)S(1)} %pad_add_fusion.idx.rest_0_, bf16[512,576]{1,0:T(8,128)(2,1)S(1)} %shard_map.91.rest_1_, s32[64]{0:T(128)S(1)} %copy-done.1, s32[64]{0:T(128)S(1)} %copy-done.2, ...), custom_call_target="tpu_custom_call" | custom-call | flops 570425344 | bytes 4194304 | tf_op jit(solution)/shard_map/pallas_call | solution.py:286
  51.9 0.0 collective-permute-done.6.rest_8_
  51.9 0.0 copy-start
  52.0 0.0 slice-start
  52.0 2.0 %shard_map.95 = (f32[512,1]{1,0:T(8,128)S(1)}, f32[512,1]{1,0:T(8,128)S(1)}, f32[512,512]{1,0:T(8,128)S(1)}) custom-call(s32[2]{0:T(128)S(1)} %pad_add_fusion.idx.rest_0_, bf16[512,576]{1,0:T(8,128)(2,1)S(1)} %shard_map.91.rest_1_, f32[4,16,512]{2,1,0:T(8,128)S(1)} %get-tuple-element.34.rest_2_, f32[512,1]{1,0:T(8,128)S(1)} %get-tuple-element.35.rest_3_, ...), custom_call_target="tpu_custom_call" | custom-call | flops 570425344 | bytes 4194304 | tf_op jit(solution)/shard_map/pallas_call | solution.py:286
  54.0 0.0 collective-permute-done.9.rest_8_
  54.0 2.0 %shard_map.96 = (f32[512,1]{1,0:T(8,128)S(1)}, f32[512,1]{1,0:T(8,128)S(1)}, f32[512,512]{1,0:T(8,128)S(1)}) custom-call(s32[2]{0:T(128)S(1)} %pad_add_fusion.idx.rest_0_, bf16[512,576]{1,0:T(8,128)(2,1)S(1)} %shard_map.91.rest_1_, f32[4,16,512]{2,1,0:T(8,128)S(1)} %get-tuple-element.34.rest_2_, f32[512,1]{1,0:T(8,128)S(1)} %get-tuple-element.38.rest_3_, ...), custom_call_target="tpu_custom_call" | custom-call | flops 570425344 | bytes 4194304 | tf_op jit(solution)/shard_map/pallas_call | solution.py:286
  56.0 0.0 slice-start.1
  56.0 1.6 %shard_map.97 = (f32[512,1]{1,0:T(8,128)S(1)}, f32[512,1]{1,0:T(8,128)S(1)}, f32[512,512]{1,0:T(8,128)S(1)}) custom-call(s32[2]{0:T(128)S(1)} %pad_add_fusion.idx.rest_0_, bf16[512,576]{1,0:T(8,128)(2,1)S(1)} %shard_map.91.rest_1_, f32[4,16,512]{2,1,0:T(8,128)S(1)} %get-tuple-element.34.rest_2_, f32[512,1]{1,0:T(8,128)S(1)} %get-tuple-element.41.rest_3_, ...), custom_call_target="tpu_custom_call" | custom-call | flops 142606336 | bytes 4194304 | tf_op jit(solution)/shard_map/pallas_call | solution.py:286
  57.7 0.0 collective-permute-done.12.rest_8_
  57.7 0.0 collective-permute-done.11.rest_7_
  57.7 2.9 %shard_map.98.rest_0_ = bf16[16,4096]{1,0:T(8,128)(2,1)S(1)} custom-call(s32[2]{0:T(128)S(1)} %pad_add_fusion.idx.rest_0_, bf16[512,576]{1,0:T(8,128)(2,1)S(1)} %shard_map.91.rest_1_, f32[4,16,512]{2,1,0:T(8,128)S(1)} %get-tuple-element.34.rest_2_, f32[512,1]{1,0:T(8,128)S(1)} %get-tuple-element.44.rest_3_, f32[512,1]{1,0:T(8,128)S(1)} %get-tuple-element.45.rest_4_, ...), custom_call_target="tpu_custom_call" | custom-call | flops 427819008 | bytes 4194304 | tf_op jit(solution)/shard_map/pallas_call | solution.py:286
  60.6 1.7 %collective-permute-start.14 = (bf16[16,4096]{1,0:T(8,128)(2,1)S(1)}, bf16[16,4096]{1,0:T(8,128)(2,1)S(1)}, u32[]{:S(2)}, u32[]{:S(2)}) collective-permute-start(bf16[16,4096]{1,0:T(8,128)(2,1)S(1)} %shard_map.98.rest_0_), channel_id=1, source_target_pairs={{0,8},{4,12},{8,0},{12,4},{16,24},{20,28},{24,16},{28,20},{1,9},{5... | collective-permute-start | bytes 393224 | tf_op jit(solution)/shard_map/ppermute | solution.py:338
  62.3 1.5 %collective-permute-start.16 = (bf16[16,4096]{1,0:T(8,128)(2,1)S(1)}, bf16[16,4096]{1,0:T(8,128)(2,1)S(1)}, u32[]{:S(2)}, u32[]{:S(2)}) collective-permute-start(bf16[16,4096]{1,0:T(8,128)(2,1)S(1)} %shard_map.98.rest_0_), channel_id=1, source_target_pairs={{0,16},{4,20},{8,24},{12,28},{16,0},{20,4},{24,8},{28,12},{1,17},{... | collective-permute-start | bytes 393224 | tf_op jit(solution)/shard_map/ppermute | solution.py:338
  63.9 0.3 collective-permute-start.18
  64.1 0.0 collective-permute-start.13
  64.1 1.7 %collective-permute-done.14.rest_2_ = bf16[16,4096]{1,0:T(8,128)(2,1)S(1)} collective-permute-done((bf16[16,4096]{1,0:T(8,128)(2,1)S(1)}, bf16[16,4096]{1,0:T(8,128)(2,1)S(1)}, u32[]{:S(2)}, u32[]{:S(2)}) %collective-permute-start.14) | collective-permute-done | bytes 131104 | tf_op jit(solution)/shard_map/ppermute | solution.py:338
  65.9 0.0 collective-permute-start.15
  65.9 1.4 %collective-permute-done.16.rest_4_ = bf16[16,4096]{1,0:T(8,128)(2,1)S(1)} collective-permute-done((bf16[16,4096]{1,0:T(8,128)(2,1)S(1)}, bf16[16,4096]{1,0:T(8,128)(2,1)S(1)}, u32[]{:S(2)}, u32[]{:S(2)}) %collective-permute-start.16) | collective-permute-done | bytes 131104 | tf_op jit(solution)/shard_map/ppermute | solution.py:338
  67.3 0.0 collective-permute-start.17
  67.3 2.4 %collective-permute-done.18.rest_6_ = bf16[16,4096]{1,0:T(8,128)(2,1)S(1)} collective-permute-done((bf16[16,4096]{1,0:T(8,128)(2,1)S(1)}, bf16[16,4096]{1,0:T(8,128)(2,1)S(1)}, u32[]{:S(2)}, u32[]{:S(2)}) %collective-permute-start.18) | collective-permute-done | bytes 131104 | tf_op jit(solution)/shard_map/ppermute | solution.py:338
  69.7 0.0 collective-permute-start.19
  69.7 0.0 collective-permute-done.13.rest_1_
  69.7 0.0 collective-permute-done.15.rest_3_
  69.7 0.0 collective-permute-done.17.rest_5_
  69.8 1.3 %collective-permute-done.19.rest_7_ = bf16[16,4096]{1,0:T(8,128)(2,1)S(1)} collective-permute-done((bf16[16,4096]{1,0:T(8,128)(2,1)S(1)}, bf16[16,4096]{1,0:T(8,128)(2,1)S(1)}, u32[]{:S(2)}, u32[]{:S(2)}) %collective-permute-start.19) | collective-permute-done | bytes 131104 | tf_op jit(solution)/shard_map/ppermute | solution.py:338
  71.1 0.0 slice-done.1
  71.1 1.9 %shard_map.99 = (f32[32,896]{1,0:T(8,128)S(1)}, bf16[32,896]{1,0:T(8,128)(2,1)S(1)}, bf16[32,896]{1,0:T(8,128)(2,1)S(1)}, bf16[32,896]{1,0:T(8,128)(2,1)S(1)}) custom-call(s32[2]{0:T(128)S(1)} %pad_add_fusion.idx.rest_0_, bf16[16,4096]{1,0:T(8,128)(2,1)S(1)} %shard_map.98.rest_0_, bf16[16,4096]{1,0:T(8,128)(2,1)S(1)} %collective-permute-done.13.rest_1_, ...), custom_call_target="tpu_custom_call" | custom-call | flops 939524096 | bytes 7340032 | tf_op jit(solution)/shard_map/pallas_call | solution.py:321
  73.0 0.1 collective-permute-start.20
  73.1 3.1 %collective-permute-start.21 = (bf16[32,896]{1,0:T(8,128)(2,1)S(1)}, bf16[32,896]{1,0:T(8,128)(2,1)S(1)}, u32[]{:S(2)}, u32[]{:S(2)}) collective-permute-start(bf16[32,896]{1,0:T(8,128)(2,1)S(1)} %get-tuple-element.49), channel_id=1, source_target_pairs={{0,2},{1,3},{2,0},{3,1},{4,6},{5,7},{6,4},{7,5},{8,10},{9,11},{10,... | collective-permute-start | bytes 172040 | tf_op jit(solution)/shard_map/ppermute | solution.py:393
  76.2 1.3 %collective-permute-start.22 = (bf16[32,896]{1,0:T(8,128)(2,1)S(1)}, bf16[32,896]{1,0:T(8,128)(2,1)S(1)}, u32[]{:S(2)}, u32[]{:S(2)}) collective-permute-start(bf16[32,896]{1,0:T(8,128)(2,1)S(1)} %get-tuple-element.50), channel_id=1, source_target_pairs={{0,3},{1,2},{2,1},{3,0},{4,7},{5,6},{6,5},{7,4},{8,11},{9,10},{10,... | collective-permute-start | bytes 172040 | tf_op jit(solution)/shard_map/ppermute | solution.py:393
  77.5 0.7 collective-permute-done.20
  78.1 1.8 %collective-permute-done.21 = bf16[32,896]{1,0:T(8,128)(2,1)S(1)} collective-permute-done((bf16[32,896]{1,0:T(8,128)(2,1)S(1)}, bf16[32,896]{1,0:T(8,128)(2,1)S(1)}, u32[]{:S(2)}, u32[]{:S(2)}) %collective-permute-start.21) | collective-permute-done | bytes 57376 | tf_op jit(solution)/shard_map/ppermute | solution.py:393
  79.9 2.3 %collective-permute-done.22 = bf16[32,896]{1,0:T(8,128)(2,1)S(1)} collective-permute-done((bf16[32,896]{1,0:T(8,128)(2,1)S(1)}, bf16[32,896]{1,0:T(8,128)(2,1)S(1)}, u32[]{:S(2)}, u32[]{:S(2)}) %collective-permute-start.22) | collective-permute-done | bytes 57376 | tf_op jit(solution)/shard_map/ppermute | solution.py:393
  82.2 0.7 add_convert_fusion
  (11 shorter events, 0.1 us)
Async XLA Ops:
  0.0 49.0 %copy-start.1 = (s32[64]{0:T(128)S(1)}, s32[64]{0:T(128)}, u32[]{:S(2)}) copy-start(s32[64]{0:T(128)} %rest_2_.1) | copy-start | bytes 772
  0.0 49.0 %copy-start.2 = (s32[64]{0:T(128)S(1)}, s32[64]{0:T(128)}, u32[]{:S(2)}) copy-start(s32[64]{0:T(128)} %rest_3_.1) | copy-start | bytes 772
  0.0 49.0 %copy-start.3 = (bf16[16,576]{1,0:T(8,128)(2,1)S(1)}, bf16[16,576]{1,0:T(8,128)(2,1)}, u32[]{:S(2)}) copy-start(bf16[16,576]{1,0:T(8,128)(2,1)} %rest_4_.1) | copy-start | bytes 55300
  1.9 1.8 %collective-permute-start = (bf16[4,64,576]{2,1,0:T(8,128)(2,1)S(1)}, bf16[4,64,576]{2,1,0:T(8,128)(2,1)S(1)}, u32[]{:S(2)}, u32[]{:S(2)}) collective-permute-start(bf16[4,64,576]{2,1,0:T(8,128)(2,1)S(1)} %get-tuple-element.29), channel_id=1, source_target_pairs={{0,4},{4,0},{8,12},{12,8},{16,20},{20,16},{24,28},{28,24},{1,5},{5... | collective-permute-start | bytes 884744 | tf_op jit(solution)/shard_map/ppermute | solution.py:338
  3.7 7.4 %collective-permute-start.1 = (bf16[2,64,576]{2,1,0:T(8,128)(2,1)S(1)}, bf16[2,64,576]{2,1,0:T(8,128)(2,1)S(1)}, u32[]{:S(2)}, u32[]{:S(2)}) collective-permute-start(bf16[2,64,576]{2,1,0:T(8,128)(2,1)S(1)} %get-tuple-element.31), channel_id=1, source_target_pairs={{0,8},{4,12},{8,0},{12,4},{16,24},{20,28},{24,16},{28,20},{1,9},{5... | collective-permute-start | bytes 442376 | tf_op jit(solution)/shard_map/ppermute | solution.py:338
  6.7 6.0 %collective-permute-start.2 = (bf16[2,64,576]{2,1,0:T(8,128)(2,1)S(1)}, bf16[2,64,576]{2,1,0:T(8,128)(2,1)S(1)}, u32[]{:S(2)}, u32[]{:S(2)}) collective-permute-start(bf16[2,64,576]{2,1,0:T(8,128)(2,1)S(1)} %get-tuple-element.32), channel_id=1, source_target_pairs={{0,16},{4,20},{8,24},{12,28},{16,0},{20,4},{24,8},{28,12},{1,17},{... | collective-permute-start | bytes 442376 | tf_op jit(solution)/shard_map/ppermute | solution.py:338
  8.2 12.4 %collective-permute-start.4 = (bf16[4,64,576]{2,1,0:T(8,128)(2,1)S(1)}, bf16[4,64,576]{2,1,0:T(8,128)(2,1)S(1)}, u32[]{:S(2)}, u32[]{:S(2)}) collective-permute-start(bf16[4,64,576]{2,1,0:T(8,128)(2,1)S(1)} %get-tuple-element.30.rest_5_), channel_id=1, source_target_pairs={{0,1},{1,2},{2,3},{3,0},{4,5},{5,6},{6,7},{7,4},{8,9},{9,10},{10,1... | collective-permute-start | bytes 884744 | tf_op jit(solution)/shard_map/ppermute | solution.py:342
  12.6 14.9 %collective-permute-start.5 = (bf16[4,64,576]{2,1,0:T(8,128)(2,1)S(1)}, bf16[4,64,576]{2,1,0:T(8,128)(2,1)S(1)}, u32[]{:S(2)}, u32[]{:S(2)}) collective-permute-start(bf16[4,64,576]{2,1,0:T(8,128)(2,1)S(1)} %constant_dynamic-update-slice_fusion.rest_6_), channel_id=1, source_target_pairs={{0,1},{1,2},{2,3},{3,0},{4,5},{5,6},{6,7},{7,4},{8,9},{9,10},{10,1... | collective-permute-start | bytes 884744 | tf_op jit(solution)/shard_map/ppermute | solution.py:342
  20.6 14.0 %collective-permute-start.7 = (bf16[4,64,576]{2,1,0:T(8,128)(2,1)S(1)}, bf16[4,64,576]{2,1,0:T(8,128)(2,1)S(1)}, u32[]{:S(2)}, u32[]{:S(2)}) collective-permute-start(bf16[4,64,576]{2,1,0:T(8,128)(2,1)S(1)} %collective-permute-done.4.rest_6_), channel_id=1, source_target_pairs={{0,1},{1,2},{2,3},{3,0},{4,5},{5,6},{6,7},{7,4},{8,9},{9,10},{10,1... | collective-permute-start | bytes 884744 | tf_op jit(solution)/shard_map/ppermute | solution.py:342
  27.6 14.0 %collective-permute-start.8 = (bf16[4,64,576]{2,1,0:T(8,128)(2,1)S(1)}, bf16[4,64,576]{2,1,0:T(8,128)(2,1)S(1)}, u32[]{:S(2)}, u32[]{:S(2)}) collective-permute-start(bf16[4,64,576]{2,1,0:T(8,128)(2,1)S(1)} %collective-permute-done.5.rest_7_), channel_id=1, source_target_pairs={{0,1},{1,2},{2,3},{3,0},{4,5},{5,6},{6,7},{7,4},{8,9},{9,10},{10,1... | collective-permute-start | bytes 884744 | tf_op jit(solution)/shard_map/ppermute | solution.py:342
  34.6 14.0 %collective-permute-start.10 = (bf16[4,64,576]{2,1,0:T(8,128)(2,1)S(1)}, bf16[4,64,576]{2,1,0:T(8,128)(2,1)S(1)}, u32[]{:S(2)}, u32[]{:S(2)}) collective-permute-start(bf16[4,64,576]{2,1,0:T(8,128)(2,1)S(1)} %collective-permute-done.7.rest_6_), channel_id=1, source_target_pairs={{0,1},{1,2},{2,3},{3,0},{4,5},{5,6},{6,7},{7,4},{8,9},{9,10},{10,1... | collective-permute-start | bytes 884744 | tf_op jit(solution)/shard_map/ppermute | solution.py:342
  34.6 14.4 %collective-permute-start.3 = (bf16[2,64,576]{2,1,0:T(8,128)(2,1)S(1)}, bf16[2,64,576]{2,1,0:T(8,128)(2,1)S(1)}, u32[]{:S(2)}, u32[]{:S(2)}) collective-permute-start(bf16[2,64,576]{2,1,0:T(8,128)(2,1)S(1)} %get-tuple-element.33), channel_id=1, source_target_pairs={{0,24},{4,28},{8,16},{12,20},{16,8},{20,12},{24,0},{28,4},{1,25},{... | collective-permute-start | bytes 442376 | tf_op jit(solution)/shard_map/ppermute | solution.py:338
  41.6 16.0 %collective-permute-start.11 = (bf16[4,64,576]{2,1,0:T(8,128)(2,1)S(1)}, bf16[4,64,576]{2,1,0:T(8,128)(2,1)S(1)}, u32[]{:S(2)}, u32[]{:S(2)}) collective-permute-start(bf16[4,64,576]{2,1,0:T(8,128)(2,1)S(1)} %collective-permute-done.8.rest_7_), channel_id=1, source_target_pairs={{0,1},{1,2},{2,3},{3,0},{4,5},{5,6},{6,7},{7,4},{8,9},{9,10},{10,1... | collective-permute-start | bytes 884744 | tf_op jit(solution)/shard_map/ppermute | solution.py:342
  41.6 10.3 %collective-permute-start.6 = (bf16[2,64,576]{2,1,0:T(8,128)(2,1)S(1)}, bf16[2,64,576]{2,1,0:T(8,128)(2,1)S(1)}, u32[]{:S(2)}, u32[]{:S(2)}) collective-permute-start(bf16[2,64,576]{2,1,0:T(8,128)(2,1)S(1)} %slice.12), channel_id=1, source_target_pairs={{0,24},{4,28},{8,16},{12,20},{16,8},{20,12},{24,0},{28,4},{1,25},{... | collective-permute-start | bytes 442376 | tf_op jit(solution)/shard_map/ppermute | solution.py:338
  42.0 12.0 %collective-permute-start.9 = (bf16[2,64,576]{2,1,0:T(8,128)(2,1)S(1)}, bf16[2,64,576]{2,1,0:T(8,128)(2,1)S(1)}, u32[]{:S(2)}, u32[]{:S(2)}) collective-permute-start(bf16[2,64,576]{2,1,0:T(8,128)(2,1)S(1)} %slice.13), channel_id=1, source_target_pairs={{0,24},{4,28},{8,16},{12,20},{16,8},{20,12},{24,0},{28,4},{1,25},{... | collective-permute-start | bytes 442376 | tf_op jit(solution)/shard_map/ppermute | solution.py:338
  48.7 9.0 %collective-permute-start.12 = (bf16[2,64,576]{2,1,0:T(8,128)(2,1)S(1)}, bf16[2,64,576]{2,1,0:T(8,128)(2,1)S(1)}, u32[]{:S(2)}, u32[]{:S(2)}) collective-permute-start(bf16[2,64,576]{2,1,0:T(8,128)(2,1)S(1)} %slice.14), channel_id=1, source_target_pairs={{0,24},{4,28},{8,16},{12,20},{16,8},{20,12},{24,0},{28,4},{1,25},{... | collective-permute-start | bytes 442376 | tf_op jit(solution)/shard_map/ppermute | solution.py:338
  51.9 5.7 %copy-start = (bf16[32,512,128]{2,1,0:T(8,128)(2,1)S(1)}, bf16[32,512,128]{2,1,0:T(8,128)(2,1)}, u32[]{:S(2)}) copy-start(bf16[32,512,128]{2,1,0:T(8,128)(2,1)} %rest_6_.1) | copy-start | bytes 12582916
  52.0 19.1 %slice-start = ((s8[7340032]{0:T(1024)(128)(4,1)}), s8[4194304]{0:T(1024)(128)(4,1)S(1)}, s32[]{:S(2)}) async-start(s8[7340032]{0:T(1024)(128)(4,1)} %bitcast.5), calls=%async_computation | async-start | bytes 8388608
  56.0 15.1 %slice-start.1 = ((s8[7340032]{0:T(1024)(128)(4,1)}), s8[3145728]{0:T(1024)(128)(4,1)S(1)}, s32[]{:S(2)}) async-start(s8[7340032]{0:T(1024)(128)(4,1)} %bitcast.5), calls=%async_computation.1 | async-start | bytes 6291456
  60.6 5.3 %collective-permute-start.14 = (bf16[16,4096]{1,0:T(8,128)(2,1)S(1)}, bf16[16,4096]{1,0:T(8,128)(2,1)S(1)}, u32[]{:S(2)}, u32[]{:S(2)}) collective-permute-start(bf16[16,4096]{1,0:T(8,128)(2,1)S(1)} %shard_map.98.rest_0_), channel_id=1, source_target_pairs={{0,8},{4,12},{8,0},{12,4},{16,24},{20,28},{24,16},{28,20},{1,9},{5... | collective-permute-start | bytes 393224 | tf_op jit(solution)/shard_map/ppermute | solution.py:338
  62.3 5.0 %collective-permute-start.16 = (bf16[16,4096]{1,0:T(8,128)(2,1)S(1)}, bf16[16,4096]{1,0:T(8,128)(2,1)S(1)}, u32[]{:S(2)}, u32[]{:S(2)}) collective-permute-start(bf16[16,4096]{1,0:T(8,128)(2,1)S(1)} %shard_map.98.rest_0_), channel_id=1, source_target_pairs={{0,16},{4,20},{8,24},{12,28},{16,0},{20,4},{24,8},{28,12},{1,17},{... | collective-permute-start | bytes 393224 | tf_op jit(solution)/shard_map/ppermute | solution.py:338
  63.9 5.9 %collective-permute-start.18 = (bf16[16,4096]{1,0:T(8,128)(2,1)S(1)}, bf16[16,4096]{1,0:T(8,128)(2,1)S(1)}, u32[]{:S(2)}, u32[]{:S(2)}) collective-permute-start(bf16[16,4096]{1,0:T(8,128)(2,1)S(1)} %shard_map.98.rest_0_), channel_id=1, source_target_pairs={{0,24},{4,28},{8,16},{12,20},{16,8},{20,12},{24,0},{28,4},{1,25},{... | collective-permute-start | bytes 393224 | tf_op jit(solution)/shard_map/ppermute | solution.py:338
  64.1 5.6 %collective-permute-start.13 = (bf16[16,4096]{1,0:T(8,128)(2,1)S(1)}, bf16[16,4096]{1,0:T(8,128)(2,1)S(1)}, u32[]{:S(2)}, u32[]{:S(2)}) collective-permute-start(bf16[16,4096]{1,0:T(8,128)(2,1)S(1)} %shard_map.98.rest_0_), channel_id=1, source_target_pairs={{0,4},{4,0},{8,12},{12,8},{16,20},{20,16},{24,28},{28,24},{1,5},{5... | collective-permute-start | bytes 393224 | tf_op jit(solution)/shard_map/ppermute | solution.py:338
  65.9 3.9 %collective-permute-start.15 = (bf16[16,4096]{1,0:T(8,128)(2,1)S(1)}, bf16[16,4096]{1,0:T(8,128)(2,1)S(1)}, u32[]{:S(2)}, u32[]{:S(2)}) collective-permute-start(bf16[16,4096]{1,0:T(8,128)(2,1)S(1)} %collective-permute-done.14.rest_2_), channel_id=1, source_target_pairs={{0,4},{4,0},{8,12},{12,8},{16,20},{20,16},{24,28},{28,24},{1,5},{5... | collective-permute-start | bytes 393224 | tf_op jit(solution)/shard_map/ppermute | solution.py:338
  67.3 2.4 %collective-permute-start.17 = (bf16[16,4096]{1,0:T(8,128)(2,1)S(1)}, bf16[16,4096]{1,0:T(8,128)(2,1)S(1)}, u32[]{:S(2)}, u32[]{:S(2)}) collective-permute-start(bf16[16,4096]{1,0:T(8,128)(2,1)S(1)} %collective-permute-done.16.rest_4_), channel_id=1, source_target_pairs={{0,4},{4,0},{8,12},{12,8},{16,20},{20,16},{24,28},{28,24},{1,5},{5... | collective-permute-start | bytes 393224 | tf_op jit(solution)/shard_map/ppermute | solution.py:338
  69.7 1.3 %collective-permute-start.19 = (bf16[16,4096]{1,0:T(8,128)(2,1)S(1)}, bf16[16,4096]{1,0:T(8,128)(2,1)S(1)}, u32[]{:S(2)}, u32[]{:S(2)}) collective-permute-start(bf16[16,4096]{1,0:T(8,128)(2,1)S(1)} %collective-permute-done.18.rest_6_), channel_id=1, source_target_pairs={{0,4},{4,0},{8,12},{12,8},{16,20},{20,16},{24,28},{28,24},{1,5},{5... | collective-permute-start | bytes 393224 | tf_op jit(solution)/shard_map/ppermute | solution.py:338
  73.0 5.1 %collective-permute-start.20 = (bf16[32,896]{1,0:T(8,128)(2,1)S(1)}, bf16[32,896]{1,0:T(8,128)(2,1)S(1)}, u32[]{:S(2)}, u32[]{:S(2)}) collective-permute-start(bf16[32,896]{1,0:T(8,128)(2,1)S(1)} %get-tuple-element.48), channel_id=1, source_target_pairs={{0,1},{1,0},{2,3},{3,2},{4,5},{5,4},{6,7},{7,6},{8,9},{9,8},{10,11... | collective-permute-start | bytes 172040 | tf_op jit(solution)/shard_map/ppermute | solution.py:393
  73.1 6.8 %collective-permute-start.21 = (bf16[32,896]{1,0:T(8,128)(2,1)S(1)}, bf16[32,896]{1,0:T(8,128)(2,1)S(1)}, u32[]{:S(2)}, u32[]{:S(2)}) collective-permute-start(bf16[32,896]{1,0:T(8,128)(2,1)S(1)} %get-tuple-element.49), channel_id=1, source_target_pairs={{0,2},{1,3},{2,0},{3,1},{4,6},{5,7},{6,4},{7,5},{8,10},{9,11},{10,... | collective-permute-start | bytes 172040 | tf_op jit(solution)/shard_map/ppermute | solution.py:393
  76.2 6.0 %collective-permute-start.22 = (bf16[32,896]{1,0:T(8,128)(2,1)S(1)}, bf16[32,896]{1,0:T(8,128)(2,1)S(1)}, u32[]{:S(2)}, u32[]{:S(2)}) collective-permute-start(bf16[32,896]{1,0:T(8,128)(2,1)S(1)} %get-tuple-element.50), channel_id=1, source_target_pairs={{0,3},{1,2},{2,1},{3,0},{4,7},{5,6},{6,5},{7,4},{8,11},{9,10},{10,... | collective-permute-start | bytes 172040 | tf_op jit(solution)/shard_map/ppermute | solution.py:393
